TPU v7x, 256 devices: a whole 4x4x8 slice. The times are simulated.
256 devices in a mesh: dp: 8 (over y, core), seq: 32 (over z, x).
Axes of the slice: x: 4, y: 4, z: 8, core: 2. Of those that a mesh axis runs over, the one named last changes fastest.
Arguments:
- queries: bfloat16 [64, 2048, 2048], P('dp', 'seq'), may hold values from -6 to 6
- enc_keys: bfloat16 [64, 2048, 2048], P('dp', 'seq'), may hold values from -6 to 6
- enc_values: bfloat16 [64, 2048, 2048], P('dp', 'seq'), may hold values from -6 to 6
- dec_ids: int32 [64, 2048], P('dp', 'seq'), may hold values from 0 to 15, never falling along the last dimension, each value on 1 to 512 neighbouring positions
- enc_ids: int32 [64, 2048], P('dp', 'seq'), may hold values from 0 to 15, never falling along the last dimension, each value on 1 to 512 neighbouring positions
Outputs:
- context: bfloat16 [64, 2048, 2048], P('dp', 'seq')
Inputs may be any that keep to these rules, and one draw needn't show every extreme that they name: `dec_ids`: along each row the numbers never fall; every number from 0 to 15 occurs in every row; a document holds 1 to 512 positions of a row, and some document holds exactly 512. `enc_ids`: along each row the numbers never fall; every number from 0 to 15 occurs in every row; a document holds 1 to 512 positions of a row, and some document holds exactly 512.
All inputs are finite; a program needn't handle non-finite values.
Results may differ from a plain program's by a relative error of at most 0.0047.
Values may be sent and summed in bfloat16 or wider, within the bound.
A program may use at most 128 MiB of HBM per device.

v0:
```python
import jax
import jax.numpy as jnp
from jax import lax
from jax.sharding import PartitionSpec as P

HEAD_DIM = 64


masked_score = -1e30


def shortened(value):

    def short(part):
        return part.astype(jnp.bfloat16) if part.dtype == jnp.float32 else part

    return jax.tree.map(short, value)


def attend_dense(query_row, key_row, value_row, dec_row, enc_row, head_count):
    length = query_row.shape[0]
    query_heads = query_row.reshape(length, head_count, HEAD_DIM)
    key_heads = key_row.reshape(length, head_count, HEAD_DIM)
    value_heads = value_row.reshape(length, head_count, HEAD_DIM)
    query_span = min(512, length)
    pieces = []
    for offset in range(0, length, query_span):
        scores = jnp.einsum(
            "qhd,khd->hqk",
            query_heads[offset : offset + query_span],
            key_heads,
            preferred_element_type=jnp.float32,
        )
        allowed = (dec_row[offset : offset + query_span][:, None] == enc_row[None, :])[None]
        scores = jnp.where(allowed, scores, masked_score)
        row_peak = jnp.max(scores, axis=2, keepdims=True)
        expos = jnp.where(allowed, jnp.exp(scores - row_peak), 0.0)
        row_total = jnp.sum(expos, axis=2, keepdims=True)
        weights = (expos / row_total).astype(jnp.bfloat16)
        summed = jnp.einsum(
            "hqk,khd->qhd", weights, value_heads, preferred_element_type=jnp.float32
        )
        pieces.append(summed.reshape(query_span, head_count * HEAD_DIM).astype(jnp.bfloat16))
    return jnp.concatenate(pieces, axis=0)


def local(queries, enc_keys, enc_values, dec_ids, enc_ids):
    group = lax.axis_size("seq")
    dec_spread = jnp.broadcast_to(
        dec_ids.astype(jnp.bfloat16)[:, :, None], (dec_ids.shape[0], dec_ids.shape[1], group)
    )
    enc_spread = jnp.broadcast_to(
        enc_ids.astype(jnp.bfloat16)[:, :, None], (enc_ids.shape[0], enc_ids.shape[1], group)
    )
    members = (
        lax.all_to_all(queries, "seq", split_axis=2, concat_axis=1, tiled=True),
        lax.all_to_all(enc_keys, "seq", split_axis=2, concat_axis=1, tiled=True),
        lax.all_to_all(enc_values, "seq", split_axis=2, concat_axis=1, tiled=True),
        lax.all_to_all(dec_spread, "seq", split_axis=2, concat_axis=1, tiled=True),
        lax.all_to_all(enc_spread, "seq", split_axis=2, concat_axis=1, tiled=True),
    )
    dec_rows = members[3][:, :, 0].astype(jnp.int32)
    enc_rows = members[4][:, :, 0].astype(jnp.int32)
    query_rows = members[0]
    key_rows = members[1]
    value_rows = members[2]
    head_count = query_rows.shape[2] // HEAD_DIM

    def one_row(members):
        return attend_dense(members[0], members[1], members[2], members[3], members[4], head_count)

    attended = lax.map(one_row, (query_rows, key_rows, value_rows, dec_rows, enc_rows))
    return lax.all_to_all(
        shortened(attended), "seq", split_axis=1, concat_axis=2, tiled=True
    ).astype(attended.dtype)


def solution(mesh):
    in_specs = (
        P("dp", "seq", None),
        P("dp", "seq", None),
        P("dp", "seq", None),
        P("dp", "seq"),
        P("dp", "seq"),
    )
    out_specs = P("dp", "seq", None)
    return jax.shard_map(local, mesh=mesh, in_specs=in_specs, out_specs=out_specs, check_vma=False)
```

profile of v0, /device:TPU:72, one launch (start us, length us, event | category | flops | bytes accessed | tf_op | source)
XLA Modules:
  0.0 455.9 jit_solution(3090840266456848962)
XLA Ops:
  1.4 10.7 %all-to-all-start.1 = ((bf16[32,2,256]{2,1,0:T(2,128)(2,1)}), bf16[32,2,256]{2,1,0:T(2,128)(2,1)S(1)}, u32[]{:S(2)}, u32[]{:S(2)}) async-start(bf16[32,2,256]{2,1,0:T(2,128)(2,1)} %reshape.168), calls=%async_computation.1 | async-start | bytes 65536 | tf_op jit(solution)/shard_map/all_to_all | solution.py:59
  13.6 6.5 %all-to-all-done.1 = bf16[32,2,256]{2,1,0:T(2,128)(2,1)S(1)} async-done(((bf16[32,2,256]{2,1,0:T(2,128)(2,1)}), bf16[32,2,256]{2,1,0:T(2,128)(2,1)S(1)}, u32[]{:S(2)}, u32[]{:S(2)}) %all-to-all-start.1) | async-done | bytes 32800 | tf_op jit(solution)/shard_map/all_to_all | solution.py:59
  20.0 5.8 %all-to-all-start.2 = ((bf16[32,2,256]{2,1,0:T(2,128)(2,1)}), bf16[32,2,256]{2,1,0:T(2,128)(2,1)S(1)}, u32[]{:S(2)}, u32[]{:S(2)}) async-start(bf16[32,2,256]{2,1,0:T(2,128)(2,1)} %reshape.170), calls=%async_computation.2 | async-start | bytes 65536 | tf_op jit(solution)/shard_map/all_to_all | solution.py:60
  25.8 5.6 %copy.18 = bf16[8,64,2048]{1,0,2:T(8,128)(2,1)} copy(bf16[8,64,2048]{2,1,0:T(8,128)(2,1)} %param.9) | data formatting | bytes 4194304 | tf_op args[2]
  31.5 7.9 %reshape.166 = bf16[32,2,16384]{2,1,0:T(2,128)(2,1)} reshape(bf16[2048,8,64]{2,1,0:T(8,128)(2,1)} %bitcast.168) | data formatting | bytes 4194304
  39.3 9.8 %all-to-all-start = ((bf16[32,2,16384]{2,1,0:T(2,128)(2,1)}), bf16[32,2,16384]{2,1,0:T(2,128)(2,1)S(1)}, u32[]{:S(2)}, u32[]{:S(2)}) async-start(bf16[32,2,16384]{2,1,0:T(2,128)(2,1)} %reshape.166), calls=%async_computation | async-start | bytes 4194304 | tf_op jit(solution)/shard_map/all_to_all | solution.py:58
  49.2 5.6 %copy.22 = bf16[8,64,2048]{1,0,2:T(8,128)(2,1)} copy(bf16[8,64,2048]{2,1,0:T(8,128)(2,1)} %param.7) | data formatting | bytes 4194304 | tf_op args[0]
  54.8 7.9 %reshape.172 = bf16[32,2,16384]{2,1,0:T(2,128)(2,1)} reshape(bf16[2048,8,64]{2,1,0:T(8,128)(2,1)} %bitcast.169) | data formatting | bytes 4194304
  62.7 35.0 %all-to-all-done = bf16[32,2,16384]{2,1,0:T(2,128)(2,1)S(1)} async-done(((bf16[32,2,16384]{2,1,0:T(2,128)(2,1)}), bf16[32,2,16384]{2,1,0:T(2,128)(2,1)S(1)}, u32[]{:S(2)}, u32[]{:S(2)}) %all-to-all-start) | async-done | bytes 2097184 | tf_op jit(solution)/shard_map/all_to_all | solution.py:58
  97.8 5.9 %all-to-all-start.3 = ((bf16[32,2,16384]{2,1,0:T(2,128)(2,1)}), bf16[32,2,16384]{2,1,0:T(2,128)(2,1)}, u32[]{:S(2)}, u32[]{:S(2)}) async-start(bf16[32,2,16384]{2,1,0:T(2,128)(2,1)} %reshape.172), calls=%async_computation.3 | async-start | bytes 4194304 | tf_op jit(solution)/shard_map/all_to_all | solution.py:56
  103.6 5.6 %copy.24 = bf16[8,64,2048]{1,0,2:T(8,128)(2,1)} copy(bf16[8,64,2048]{2,1,0:T(8,128)(2,1)} %param.8) | data formatting | bytes 4194304 | tf_op args[1]
  109.3 7.9 %reshape.174 = bf16[32,2,16384]{2,1,0:T(2,128)(2,1)} reshape(bf16[2048,8,64]{2,1,0:T(8,128)(2,1)} %bitcast.170) | data formatting | bytes 4194304
  117.2 34.2 %all-to-all-done.3 = bf16[32,2,16384]{2,1,0:T(2,128)(2,1)} async-done(((bf16[32,2,16384]{2,1,0:T(2,128)(2,1)}), bf16[32,2,16384]{2,1,0:T(2,128)(2,1)}, u32[]{:S(2)}, u32[]{:S(2)}) %all-to-all-start.3) | async-done | bytes 2097184 | tf_op jit(solution)/shard_map/all_to_all | solution.py:56
  151.4 5.9 %all-to-all-start.4 = ((bf16[32,2,16384]{2,1,0:T(2,128)(2,1)}), bf16[32,2,16384]{2,1,0:T(2,128)(2,1)}, u32[]{:S(2)}, u32[]{:S(2)}) async-start(bf16[32,2,16384]{2,1,0:T(2,128)(2,1)} %reshape.174), calls=%async_computation.4 | async-start | bytes 4194304 | tf_op jit(solution)/shard_map/all_to_all | solution.py:57
  157.8 4.0 reshape.167
  161.9 6.7 %copy.19 = bf16[8,32,64,64]{3,2,1,0:T(8,128)(2,1)} copy(bf16[8,32,64,64]{2,0,3,1:T(8,128)(2,1)} %bitcast.171) | data formatting | bytes 4194304 | tf_op jit(solution)/shard_map/all_to_all | solution.py:58
  168.5 8.0 %reshape.173 = bf16[2048,8,64]{2,1,0:T(8,128)(2,1)} reshape(bf16[32,2,16384]{2,1,0:T(2,128)(2,1)} %all-to-all-done.3) | data formatting | bytes 4194304
  176.5 6.7 %copy.23 = bf16[8,32,64,64]{3,2,1,0:T(8,128)(2,1)} copy(bf16[8,32,64,64]{2,0,3,1:T(8,128)(2,1)} %bitcast.172) | data formatting | bytes 4194304 | tf_op jit(solution)/shard_map/all_to_all | solution.py:56
  183.2 21.7 %all-to-all-done.4 = bf16[32,2,16384]{2,1,0:T(2,128)(2,1)} async-done(((bf16[32,2,16384]{2,1,0:T(2,128)(2,1)}), bf16[32,2,16384]{2,1,0:T(2,128)(2,1)}, u32[]{:S(2)}, u32[]{:S(2)}) %all-to-all-start.4) | async-done | bytes 2097184 | tf_op jit(solution)/shard_map/all_to_all | solution.py:57
  204.9 8.0 %reshape.175 = bf16[2048,8,64]{2,1,0:T(8,128)(2,1)} reshape(bf16[32,2,16384]{2,1,0:T(2,128)(2,1)} %all-to-all-done.4) | data formatting | bytes 4194304
  212.9 6.8 %copy.25 = bf16[8,32,64,64]{3,2,1,0:T(8,128)(2,1)} copy(bf16[8,32,64,64]{2,0,3,1:T(8,128)(2,1)} %bitcast.173) | data formatting | bytes 4194304 | tf_op jit(solution)/shard_map/all_to_all | solution.py:57
  219.7 150.6 %while.10 = (s32[]{:T(128)}, bf16[8,2048,64]{1,2,0:T(8,128)(2,1)S(1)}, bf16[8,2048,64]{2,1,0:T(8,128)(2,1)}, s32[8,2048]{1,0:T(8,128)S(1)}, s32[8,2048]{1,0:T(8,...) while((s32[]{:T(128)}, ...), condition=%wide.region_9.10_spmd, body=%wide.region_0.9_spmd.sunk | while | flops 1133637632 | bytes 72773864 | solution.py:72
  225.5 3.9 fusion.85
  244.3 3.9 fusion.85
  263.1 3.9 fusion.85
  281.9 3.9 fusion.85
  370.3 4.3 copy.26
  374.6 6.9 %reshape.176 = bf16[32,2,16384]{2,1,0:T(2,128)(2,1)S(1)} reshape(bf16[2048,8,64]{2,1,0:T(8,128)(2,1)} %bitcast.167) | data formatting | bytes 4194304
  381.5 52.8 %all_to_all.90 = bf16[32,2,16384]{2,1,0:T(2,128)(2,1)} all-to-all(bf16[32,2,16384]{2,1,0:T(2,128)(2,1)S(1)} %reshape.176), channel_id=1, replica_groups=mesh['dp'=8,'seq'=32] {'seq'}, dimensions={0} | all-to-all | bytes 4194304 | tf_op jit(solution)/shard_map/all_to_all | solution.py:73
  434.4 7.9 %reshape.177 = bf16[2048,8,64]{2,1,0:T(8,128)(2,1)} reshape(bf16[32,2,16384]{2,1,0:T(2,128)(2,1)} %all_to_all.90) | data formatting | bytes 4194304
  442.3 6.9 %copy.27 = bf16[8,64,32,64]{3,2,1,0:T(8,128)(2,1)} copy(bf16[8,64,32,64]{3,0,1,2:T(8,128)(2,1)} %bitcast.174) | data formatting | bytes 4194304 | tf_op jit(solution)/shard_map/all_to_all | solution.py:73
  449.2 6.7 %all_to_all.83 = bf16[8,64,2048]{2,1,0:T(8,128)(2,1)} reshape(bf16[8,64,32,64]{3,2,1,0:T(8,128)(2,1)} %copy.27) | data formatting | bytes 4194304 | tf_op jit(solution)/shard_map/all_to_all | solution.py:73
  (126 shorter events, 138.0 us)
Async XLA Ops:
  1.4 18.6 %all-to-all-start.1 = ((bf16[32,2,256]{2,1,0:T(2,128)(2,1)}), bf16[32,2,256]{2,1,0:T(2,128)(2,1)S(1)}, u32[]{:S(2)}, u32[]{:S(2)}) async-start(bf16[32,2,256]{2,1,0:T(2,128)(2,1)} %reshape.168), calls=%async_computation.1 | async-start | bytes 65536 | tf_op jit(solution)/shard_map/all_to_all | solution.py:59
  20.0 19.3 %all-to-all-start.2 = ((bf16[32,2,256]{2,1,0:T(2,128)(2,1)}), bf16[32,2,256]{2,1,0:T(2,128)(2,1)S(1)}, u32[]{:S(2)}, u32[]{:S(2)}) async-start(bf16[32,2,256]{2,1,0:T(2,128)(2,1)} %reshape.170), calls=%async_computation.2 | async-start | bytes 65536 | tf_op jit(solution)/shard_map/all_to_all | solution.py:60
  39.3 58.4 %all-to-all-start = ((bf16[32,2,16384]{2,1,0:T(2,128)(2,1)}), bf16[32,2,16384]{2,1,0:T(2,128)(2,1)S(1)}, u32[]{:S(2)}, u32[]{:S(2)}) async-start(bf16[32,2,16384]{2,1,0:T(2,128)(2,1)} %reshape.166), calls=%async_computation | async-start | bytes 4194304 | tf_op jit(solution)/shard_map/all_to_all | solution.py:58
  97.8 53.6 %all-to-all-start.3 = ((bf16[32,2,16384]{2,1,0:T(2,128)(2,1)}), bf16[32,2,16384]{2,1,0:T(2,128)(2,1)}, u32[]{:S(2)}, u32[]{:S(2)}) async-start(bf16[32,2,16384]{2,1,0:T(2,128)(2,1)} %reshape.172), calls=%async_computation.3 | async-start | bytes 4194304 | tf_op jit(solution)/shard_map/all_to_all | solution.py:56
  151.4 53.5 %all-to-all-start.4 = ((bf16[32,2,16384]{2,1,0:T(2,128)(2,1)}), bf16[32,2,16384]{2,1,0:T(2,128)(2,1)}, u32[]{:S(2)}, u32[]{:S(2)}) async-start(bf16[32,2,16384]{2,1,0:T(2,128)(2,1)} %reshape.174), calls=%async_computation.4 | async-start | bytes 4194304 | tf_op jit(solution)/shard_map/all_to_all | solution.py:57
  212.9 6.9 %copy-start.1 = (bf16[8,2048,64]{1,2,0:T(8,128)(2,1)S(1)}, bf16[8,2048,64]{1,2,0:T(8,128)(2,1)}, u32[]{:S(2)}) copy-start(bf16[8,2048,64]{1,2,0:T(8,128)(2,1)} %custom-call) | copy-start | bytes 6291460
  225.4 3.9 copy-start
  244.3 3.9 copy-start
  263.1 3.9 copy-start
  281.9 3.9 copy-start
  300.8 3.9 copy-start
  319.6 3.9 copy-start
  338.4 3.9 copy-start
  357.3 3.9 copy-start
where the time goes:
time: 460 us; the launch traced here: 456 us
  matrix products  122 us (27%)
  local copies, waits for them, and re-layouts  116 us (25%)
  waiting for transfers between devices  97.4 us (21%)
  blocking collectives  52.8 us (11%)
  starting transfers between devices  38.1 us (8%)
  other arithmetic  29 us (6%)
    unnamed x19, local copies, waits for them, and re-layouts  77 us
    dot_general x32, matrix products, attend_dense(): jnp.einsum('qhd,khd->hqk', query_heads[offset:offset + query_span], key_h...  75.8 us
    all_to_all x1, blocking collectives, local(): lax.all_to_all(shortened(attended), 'seq', split_axis=1, concat_axis=2, t...  52.8 us
    dot_general x32, matrix products, attend_dense(): jnp.einsum('hqk,khd->qhd', weights, value_heads, preferred_element_type=j...  45.8 us
    all_to_all x1, waiting for transfers between devices, local(): lax.all_to_all(enc_values, 'seq', split_axis=2, concat_axis=1, tiled=True)  35 us
    all_to_all x1, waiting for transfers between devices, local(): lax.all_to_all(queries, 'seq', split_axis=2, concat_axis=1, tiled=True)  34.2 us
    reduce_sum x8, other arithmetic, attend_dense(): row_total = jnp.sum(expos, axis=2, keepdims=True)  27.4 us
    all_to_all x1, waiting for transfers between devices, local(): lax.all_to_all(enc_keys, 'seq', split_axis=2, concat_axis=1, tiled=True)  21.7 us
  transfers between devices with their start and end apart: 5, of which 4 were waited for; matrix products, arithmetic and copies ran while one was open for 15% of the time, Pallas kernels for 0%

commit v1 on v0

v1 whole, which is shorter than its diff:
```python
import functools

import jax
import jax.numpy as jnp
from jax import lax
from jax.experimental import pallas as pl
from jax.experimental.pallas import tpu as pltpu
from jax.sharding import PartitionSpec as P

HEAD_DIM = 64
LANES = 128
NDOC = 16
FAR = -float(2**30)
MESH = pl.DeviceIdType.MESH


def doc_counts(ids, base, lane):
    counts = jnp.zeros((ids.shape[0], LANES), jnp.int32)
    slot = lane % HEAD_DIM
    for d in range(NDOC + 1):
        below = jnp.sum(jnp.where(ids < d, 1, 0), axis=1, keepdims=True)
        counts = jnp.where(slot == base + d, below, counts)
    return counts


def kernel(
    size, q_ref, k_ref, v_ref, dec_ref, enc_ref, out_ref,
    q_buf, k_buf, v_buf, o_buf, k_aug, cnt, gath, edges,
    send_sem, recv_sem, cnt_send_sem, cnt_sem, out_send_sem, out_sem,
):
    me = lax.axis_index("seq")
    rows, span = q_buf.shape[0], q_ref.shape[1]
    length = q_buf.shape[1]
    block = min(256, length)
    per_block = block // span
    n_blocks = length // block
    my_pair, my_half = me // 2, lax.rem(me, 2)

    def other(o):
        return lax.rem(me + o, size)

    def lanes_of(t):
        return pl.ds(pl.multiple_of((t // 2) * LANES, LANES), LANES)

    def span_of(t):
        return pl.ds(pl.multiple_of(t * span, span), span)

    barrier = pltpu.get_barrier_semaphore()

    def greet(o, carry):
        pl.semaphore_signal(barrier, inc=1, device_id={"seq": other(o)}, device_id_type=MESH)
        return carry

    lax.fori_loop(1, size, greet, 0)

    arrays = ((k_ref, k_buf), (q_ref, q_buf), (v_ref, v_buf))

    def landing(buf, r, where):
        return buf.at[r, where, pl.ds(0, LANES)]

    for r in range(rows):
        for a, (src, dst) in enumerate(arrays):
            pltpu.make_async_copy(
                src.at[my_half * rows + r, :, lanes_of(me)],
                landing(dst, r, span_of(me)),
                recv_sem.at[r, a],
            ).start()

    lane8 = lax.broadcasted_iota(jnp.int32, (2 * rows, LANES), 1)
    counts = doc_counts(dec_ref[...], 0, lane8) + doc_counts(enc_ref[...], 32, lane8)
    cnt[0] = counts[:rows]
    cnt[1] = counts[rows:]
    gath[me] = jnp.where(my_half == 0, counts[:rows], counts[rows:])
    v_buf[:, :, LANES:] = jnp.ones((rows, length, LANES), jnp.bfloat16)

    pl.semaphore_wait(barrier, size - 1)

    def send_counts(o, carry):
        t = other(o)
        pltpu.make_async_remote_copy(
            src_ref=cnt.at[lax.rem(t, 2)], dst_ref=gath.at[me],
            send_sem=cnt_send_sem, recv_sem=cnt_sem, device_id={"seq": t}, device_id_type=MESH,
        ).start()
        return carry

    lax.fori_loop(1, size, send_counts, 0)

    for r in range(rows):
        for a, (src, dst) in enumerate(arrays):
            def send(o, carry, r=r, a=a, src=src, dst=dst):
                t = other(o)
                pltpu.make_async_remote_copy(
                    src_ref=src.at[lax.rem(t, 2) * rows + r, :, lanes_of(t)],
                    dst_ref=landing(dst, r, span_of(me)),
                    send_sem=send_sem.at[r, a], recv_sem=recv_sem.at[r, a],
                    device_id={"seq": t}, device_id_type=MESH,
                ).start()
                return carry

            lax.fori_loop(1, size, send, 0)

    others = gath.at[pl.ds(0, size - 1)]
    pltpu.make_async_copy(others, others, cnt_sem).wait()
    total = jnp.sum(gath[...], axis=0)
    lane4 = lax.broadcasted_iota(jnp.int32, (rows, LANES), 1)
    real = lane4 % HEAD_DIM < NDOC
    encs = pltpu.roll(total, LANES - 32, 1)
    edges[0] = jnp.where(real, total, 2 * length)
    edges[1] = jnp.where(real, pltpu.roll(total, LANES - 1, 1), 0)
    edges[2] = jnp.where(real, encs, 2 * length)
    edges[3] = jnp.where(real, pltpu.roll(encs, LANES - 1, 1), 0)

    def inside(first, r, start, count):
        pos = lax.broadcasted_iota(jnp.int32, (count, LANES), 0) + start
        low = edges[first, pl.ds(r, 1), :]
        high = edges[first + 1, pl.ds(r, 1), :]
        return (pos >= low) & (pos < high)

    def out_copies(r, blk):
        for i in range(per_block):
            t = blk * per_block + i
            src = o_buf.at[r, span_of(t), :]
            dst = out_ref.at[my_half * rows + r, :, lanes_of(me)]

            @pl.when(t != me)
            def _():
                pltpu.make_async_remote_copy(
                    src_ref=src, dst_ref=dst, send_sem=out_send_sem.at[r], recv_sem=out_sem,
                    device_id={"seq": t}, device_id_type=MESH,
                ).start()

            @pl.when(t == me)
            def _():
                pltpu.make_async_copy(src, dst, out_sem).start()

    left = lax.broadcasted_iota(jnp.int32, (block, LANES), 1) < HEAD_DIM

    def attend_row(r, carry):
        for a, (_, dst) in enumerate(arrays):
            here = landing(dst, r, pl.ds(0, length))
            pltpu.make_async_copy(here, here, recv_sem.at[r, a]).wait()

        def widen(c, inner):
            at = pl.ds(pl.multiple_of(c * block, block), block)
            keys = k_buf[r, at, :]
            apart = jnp.where(inside(2, r, c * block, block), 0.0, FAR).astype(jnp.bfloat16)
            k_aug[0, at, :] = jnp.where(left, keys, apart)
            k_aug[1, at, :] = jnp.where(left, apart, keys)
            return inner

        lax.fori_loop(0, n_blocks, widen, 0)

        def attend_block(blk, inner):
            at = pl.ds(pl.multiple_of(blk * block, block), block)
            mine = q_buf[r, at, :]
            member = jnp.where(inside(0, r, blk * block, block), 1.0, 0.0).astype(jnp.bfloat16)
            values = v_buf[r]
            heads = []
            for h in range(2):
                ask = jnp.where(left, mine, member) if h == 0 else jnp.where(left, member, mine)
                scores = lax.dot_general(
                    ask, k_aug[h], (((1,), (1,)), ((), ())), preferred_element_type=jnp.float32
                )
                peak = jnp.max(scores, axis=1, keepdims=True)
                expos = jnp.exp(scores - peak).astype(jnp.bfloat16)
                summed = jnp.dot(expos, values, preferred_element_type=jnp.float32)
                heads.append(summed[:, :LANES] / summed[:, LANES:])
            o_buf[r, at, :] = jnp.where(left, heads[0], heads[1]).astype(jnp.bfloat16)

            @pl.when(blk > 0)
            def _():
                out_copies(r, blk - 1)

            return inner

        lax.fori_loop(0, n_blocks, attend_block, 0)
        out_copies(r, n_blocks - 1)
        return carry

    lax.fori_loop(0, rows, attend_row, 0)

    pltpu.make_async_copy(others, others, cnt_send_sem).wait()
    for r in range(rows):
        for a, (_, dst) in enumerate(arrays):
            most = landing(dst, r, pl.ds(0, length - span))
            pltpu.make_async_copy(most, most, send_sem.at[r, a]).wait()
        most = o_buf.at[r, pl.ds(0, length - span), :]
        pltpu.make_async_copy(most, most, out_send_sem.at[r]).wait()
    pltpu.make_async_copy(out_ref, out_ref, out_sem).wait()


def local(queries, enc_keys, enc_values, dec_ids, enc_ids):
    size = lax.axis_size("seq")
    batch, span, inner = queries.shape
    rows, length = batch // 2, span * size
    anywhere = pl.BlockSpec(memory_space=pl.ANY)
    vmem = pl.BlockSpec(memory_space=pltpu.VMEM)
    return pl.pallas_call(
        functools.partial(kernel, size),
        out_shape=jax.ShapeDtypeStruct(queries.shape, queries.dtype),
        in_specs=[anywhere, anywhere, anywhere, vmem, vmem],
        out_specs=anywhere,
        scratch_shapes=[
            pltpu.VMEM((rows, length, LANES), jnp.bfloat16),
            pltpu.VMEM((rows, length, LANES), jnp.bfloat16),
            pltpu.VMEM((rows, length, 2 * LANES), jnp.bfloat16),
            pltpu.VMEM((rows, length, LANES), jnp.bfloat16),
            pltpu.VMEM((2, length, LANES), jnp.bfloat16),
            pltpu.VMEM((2, rows, LANES), jnp.int32),
            pltpu.VMEM((size, rows, LANES), jnp.int32),
            pltpu.VMEM((4, rows, LANES), jnp.int32),
            pltpu.SemaphoreType.DMA((rows, 3)),
            pltpu.SemaphoreType.DMA((rows, 3)),
            pltpu.SemaphoreType.DMA,
            pltpu.SemaphoreType.DMA,
            pltpu.SemaphoreType.DMA((rows,)),
            pltpu.SemaphoreType.DMA,
        ],
        compiler_params=pltpu.CompilerParams(
            collective_id=0, has_side_effects=True, vmem_limit_bytes=60 * 1024 * 1024
        ),
    )(queries, enc_keys, enc_values, dec_ids, enc_ids)


def solution(mesh):
    spec, id_spec = P("dp", "seq", None), P("dp", "seq")
    return jax.shard_map(
        local, mesh=mesh, in_specs=(spec, spec, spec, id_spec, id_spec), out_specs=spec, check_vma=False
    )
```

time: 460 us -> 195 us (0.42)
  Pallas kernels: 0 us -> 192 us
  matrix products: 122 us -> 0 us
  local copies, waits for them, and re-layouts: 116 us -> 3.16 us
  waiting for transfers between devices: 97.4 us -> 0 us
  blocking collectives: 52.8 us -> 0 us
  starting transfers between devices: 38.1 us -> 0 us
  other arithmetic: 29 us -> 0 us
    pallas_call x0 -> x1, Pallas kernels: none -> 192 us  [local(): pl.pallas_call(functools.partial(kernel, size), out_shape=jax.ShapeDtypeS...]
    dot_general x64 -> x0, matrix products: 122 us -> none  [the longest x32 75.8 us: attend_dense(): jnp.einsum('qhd,khd->hqk', query_heads[offset:offset + query_span], key_h...]
    all_to_all x5 -> x0, waiting for transfers between devices: 97.4 us -> none  [the longest x1 35 us: local(): lax.all_to_all(enc_values, 'seq', split_axis=2, concat_axis=1, tiled=True)]
    unnamed x19 -> x1, local copies, waits for them, and re-layouts: 77 us -> 3.16 us
    all_to_all x1 -> x0, blocking collectives: 52.8 us -> none  [local(): lax.all_to_all(shortened(attended), 'seq', split_axis=1, concat_axis=2, t...]
    all_to_all x5 -> x0, starting transfers between devices: 38.1 us -> none  [the longest x1 10.7 us: local(): lax.all_to_all(dec_spread, 'seq', split_axis=2, concat_axis=1, tiled=True)]
    all_to_all x5 -> x0, local copies, waits for them, and re-layouts: 33.8 us -> none  [the longest x2 13.6 us: local(): lax.all_to_all(shortened(attended), 'seq', split_axis=1, concat_axis=2, t...]
    reduce_sum x8 -> x0, other arithmetic: 27.4 us -> none  [attend_dense(): row_total = jnp.sum(expos, axis=2, keepdims=True)]
  transfers between devices with their start and end apart: 5 -> 0, of which waited for: 4 -> 0; matrix products, arithmetic and copies ran while one was open for 15% -> 0% of each run, Pallas kernels for 0% -> 0%
where the time goes in v1:
time: 195 us
  Pallas kernels  192 us (98%)
  local copies, waits for them, and re-layouts  3.16 us (2%)
    pallas_call x1, Pallas kernels, local(): pl.pallas_call(functools.partial(kernel, size), out_shape=jax.ShapeDtypeS...  192 us

profile of v1, /device:TPU:72, one launch (start us, length us, event | category | flops | bytes accessed | tf_op | source)
XLA Modules:
  0.0 195.3 jit_solution(15658982366656670457)
XLA Ops:
  0.0 192.1 %shard_map.55 = bf16[8,64,2048]{2,1,0:T(8,128)(2,1)} custom-call(bf16[8,64,2048]{2,1,0:T(8,128)(2,1)} %q_ref.1, bf16[8,64,2048]{2,1,0:T(8,128)(2,1)} %k_ref.1, bf16[8,64,2048]{2,1,0:T(8,128)(2,1)} %v_ref.1, s32[8,64]{1,0:T(8,128)} %dec_ref.1, s32[8,64]{1,0:T(8,128)} %enc_ref.1), custom_call_target="tpu_custom_call" | custom-call | tf_op jit(solution)/shard_map/pallas_call | solution.py:198
  192.2 3.2 %copy.7 = bf16[8,64,2048]{2,1,0:T(8,128)(2,1)} copy(bf16[8,64,2048]{2,1,0:T(8,128)(2,1)} %shard_map.55) | data formatting | bytes 4194304

commit v2 on v1

--- a/solution.py
+++ b/solution.py
@@ -10,14 +10,14 @@
 HEAD_DIM = 64
 LANES = 128
 NDOC = 16
+RING_X = 4
 FAR = -float(2**30)
 MESH = pl.DeviceIdType.MESH
 
 
-def doc_counts(ids, base, lane):
+def doc_counts(ids, base, slot):
     counts = jnp.zeros((ids.shape[0], LANES), jnp.int32)
-    slot = lane % HEAD_DIM
-    for d in range(NDOC + 1):
+    for d in range(1, NDOC):
         below = jnp.sum(jnp.where(ids < d, 1, 0), axis=1, keepdims=True)
         counts = jnp.where(slot == base + d, below, counts)
     return counts
@@ -26,7 +26,7 @@
 def kernel(
     size, q_ref, k_ref, v_ref, dec_ref, enc_ref, out_ref,
     q_buf, k_buf, v_buf, o_buf, k_aug, cnt, gath, edges,
-    send_sem, recv_sem, cnt_send_sem, cnt_sem, out_send_sem, out_sem,
+    send_sem, recv_sem, cnt_send_sem, cnt_sem, out_send_sem, out_sem, round_sem,
 ):
     me = lax.axis_index("seq")
     rows, span = q_buf.shape[0], q_ref.shape[1]
@@ -34,10 +34,8 @@
     block = min(256, length)
     per_block = block // span
     n_blocks = length // block
-    my_pair, my_half = me // 2, lax.rem(me, 2)
-
-    def other(o):
-        return lax.rem(me + o, size)
+    my_half = lax.rem(me, 2)
+    ring_z, rounds = size // RING_X, round_sem.shape[0]
 
     def lanes_of(t):
         return pl.ds(pl.multiple_of((t // 2) * LANES, LANES), LANES)
@@ -45,13 +43,17 @@
     def span_of(t):
         return pl.ds(pl.multiple_of(t * span, span), span)
 
+    def place(dz, dx):
+        return lax.rem(me // RING_X + dz, ring_z) * RING_X + lax.rem(lax.rem(me, RING_X) + dx, RING_X)
+
+    neighbours = (place(1, 0), place(ring_z - 1, 0), place(0, 1), place(0, RING_X - 1))
+
+    def greet(sem):
+        for t in neighbours:
+            pl.semaphore_signal(sem, inc=1, device_id={"seq": t}, device_id_type=MESH)
+
     barrier = pltpu.get_barrier_semaphore()
-
-    def greet(o, carry):
-        pl.semaphore_signal(barrier, inc=1, device_id={"seq": other(o)}, device_id_type=MESH)
-        return carry
-
-    lax.fori_loop(1, size, greet, 0)
+    greet(barrier)
 
     arrays = ((k_ref, k_buf), (q_ref, q_buf), (v_ref, v_buf))
 
@@ -67,48 +69,83 @@
             ).start()
 
     lane8 = lax.broadcasted_iota(jnp.int32, (2 * rows, LANES), 1)
-    counts = doc_counts(dec_ref[...], 0, lane8) + doc_counts(enc_ref[...], 32, lane8)
-    cnt[0] = counts[:rows]
-    cnt[1] = counts[rows:]
-    gath[me] = jnp.where(my_half == 0, counts[:rows], counts[rows:])
-    v_buf[:, :, LANES:] = jnp.ones((rows, length, LANES), jnp.bfloat16)
-
-    pl.semaphore_wait(barrier, size - 1)
-
-    def send_counts(o, carry):
-        t = other(o)
+    row8 = lax.broadcasted_iota(jnp.int32, (2 * rows, LANES), 0)
+    counts = doc_counts(dec_ref[...], 0, lane8 % (2 * NDOC)) + doc_counts(enc_ref[...], NDOC, lane8 % (2 * NDOC))
+    for half in range(2):
+        kept = (row8 // rows == half) & (lane8 // (2 * NDOC) == row8 % rows)
+        line = jnp.sum(jnp.where(kept, counts, 0), axis=0, keepdims=True)
+        cnt[half] = line
+
+        @pl.when(my_half == half)
+        def _():
+            gath[me] = line
+    def send_counts(t):
         pltpu.make_async_remote_copy(
             src_ref=cnt.at[lax.rem(t, 2)], dst_ref=gath.at[me],
             send_sem=cnt_send_sem, recv_sem=cnt_sem, device_id={"seq": t}, device_id_type=MESH,
         ).start()
-        return carry
-
-    lax.fori_loop(1, size, send_counts, 0)
-
-    for r in range(rows):
-        for a, (src, dst) in enumerate(arrays):
-            def send(o, carry, r=r, a=a, src=src, dst=dst):
-                t = other(o)
-                pltpu.make_async_remote_copy(
-                    src_ref=src.at[lax.rem(t, 2) * rows + r, :, lanes_of(t)],
-                    dst_ref=landing(dst, r, span_of(me)),
-                    send_sem=send_sem.at[r, a], recv_sem=recv_sem.at[r, a],
-                    device_id={"seq": t}, device_id_type=MESH,
-                ).start()
-                return carry
-
-            lax.fori_loop(1, size, send, 0)
+
+    def send(t, r, a):
+        src, dst = arrays[a]
+        pltpu.make_async_remote_copy(
+            src_ref=src.at[lax.rem(t, 2) * rows + r, :, lanes_of(t)],
+            dst_ref=landing(dst, r, span_of(me)),
+            send_sem=send_sem.at[r, a], recv_sem=recv_sem.at[r, a],
+            device_id={"seq": t}, device_id_type=MESH,
+        ).start()
+
+    def each_at(nearest, farthest, act):
+        def step(o, carry):
+            dz, dx = o // RING_X, lax.rem(o, RING_X)
+            hops = jnp.minimum(dz, ring_z - dz) + jnp.minimum(dx, RING_X - dx)
+
+            @pl.when((hops >= nearest) & (hops <= farthest))
+            def _():
+                act(place(dz, dx))
+
+            return carry
+
+        lax.fori_loop(1, size, step, 0)
+
+    def send_row(r, nearest, farthest):
+        for a in range(3):
+            each_at(nearest, farthest, lambda t: send(t, r, a))
+
+    pl.semaphore_wait(barrier, 4)
+    greet(round_sem.at[0])
+    for t in neighbours:
+        send_counts(t)
+    for r in range(rows):
+        for a in range(3):
+            for t in neighbours:
+                send(t, r, a)
+    pl.semaphore_wait(round_sem.at[0], 4)
+    greet(round_sem.at[1])
+    each_at(2, 2, send_counts)
+    send_row(0, 2, 2)
+    for k in range(1, rounds):
+        pl.semaphore_wait(round_sem.at[k], 4)
+        if k + 1 < rounds:
+            greet(round_sem.at[k + 1])
+    each_at(3, size, send_counts)
+    send_row(0, 3, size)
+    for r in range(1, rows):
+        send_row(r, 2, size)
+    v_buf[:, :, LANES:] = jnp.ones((rows, length, LANES), jnp.bfloat16)
 
     others = gath.at[pl.ds(0, size - 1)]
     pltpu.make_async_copy(others, others, cnt_sem).wait()
-    total = jnp.sum(gath[...], axis=0)
-    lane4 = lax.broadcasted_iota(jnp.int32, (rows, LANES), 1)
-    real = lane4 % HEAD_DIM < NDOC
-    encs = pltpu.roll(total, LANES - 32, 1)
-    edges[0] = jnp.where(real, total, 2 * length)
-    edges[1] = jnp.where(real, pltpu.roll(total, LANES - 1, 1), 0)
-    edges[2] = jnp.where(real, encs, 2 * length)
-    edges[3] = jnp.where(real, pltpu.roll(encs, LANES - 1, 1), 0)
+    total = jnp.broadcast_to(jnp.sum(gath[...], axis=0), (8, LANES))
+    slot = lax.broadcasted_iota(jnp.int32, (8, LANES), 1)
+    for r in range(rows):
+        for which in range(2):
+            base = (2 * r + which) * NDOC
+            low = pltpu.roll(total, (LANES - base) % LANES, 1)
+            low = jnp.where(slot < HEAD_DIM, low, pltpu.roll(low, HEAD_DIM, 1))
+            high = jnp.where(slot % HEAD_DIM == NDOC - 1, length, pltpu.roll(low, LANES - 1, 1))
+            real = slot % HEAD_DIM < NDOC
+            edges[2 * which, pl.ds(r, 1), :] = jnp.where(real, low, 2 * length)[:1]
+            edges[2 * which + 1, pl.ds(r, 1), :] = jnp.where(real, high, 0)[:1]
 
     def inside(first, r, start, count):
         pos = lax.broadcasted_iota(jnp.int32, (count, LANES), 0) + start
@@ -131,7 +168,7 @@
 
             @pl.when(t == me)
             def _():
-                pltpu.make_async_copy(src, dst, out_sem).start()
+                out_ref[my_half * rows + r, :, lanes_of(me)] = o_buf[r, span_of(me), :]
 
     left = lax.broadcasted_iota(jnp.int32, (block, LANES), 1) < HEAD_DIM
 
@@ -186,7 +223,8 @@
             pltpu.make_async_copy(most, most, send_sem.at[r, a]).wait()
         most = o_buf.at[r, pl.ds(0, length - span), :]
         pltpu.make_async_copy(most, most, out_send_sem.at[r]).wait()
-    pltpu.make_async_copy(out_ref, out_ref, out_sem).wait()
+    came = o_buf.at[:, pl.ds(0, length - span), :]
+    pltpu.make_async_copy(came, came, out_sem).wait()
 
 
 def local(queries, enc_keys, enc_values, dec_ids, enc_ids):
@@ -197,17 +235,17 @@
     vmem = pl.BlockSpec(memory_space=pltpu.VMEM)
     return pl.pallas_call(
         functools.partial(kernel, size),
-        out_shape=jax.ShapeDtypeStruct(queries.shape, queries.dtype),
+        out_shape=pltpu.VMEM(queries.shape, queries.dtype),
         in_specs=[anywhere, anywhere, anywhere, vmem, vmem],
-        out_specs=anywhere,
+        out_specs=vmem,
         scratch_shapes=[
             pltpu.VMEM((rows, length, LANES), jnp.bfloat16),
             pltpu.VMEM((rows, length, LANES), jnp.bfloat16),
             pltpu.VMEM((rows, length, 2 * LANES), jnp.bfloat16),
             pltpu.VMEM((rows, length, LANES), jnp.bfloat16),
             pltpu.VMEM((2, length, LANES), jnp.bfloat16),
-            pltpu.VMEM((2, rows, LANES), jnp.int32),
-            pltpu.VMEM((size, rows, LANES), jnp.int32),
+            pltpu.VMEM((2, 1, LANES), jnp.int32),
+            pltpu.VMEM((size, 1, LANES), jnp.int32),
             pltpu.VMEM((4, rows, LANES), jnp.int32),
             pltpu.SemaphoreType.DMA((rows, 3)),
             pltpu.SemaphoreType.DMA((rows, 3)),
@@ -215,9 +253,10 @@
             pltpu.SemaphoreType.DMA,
             pltpu.SemaphoreType.DMA((rows,)),
             pltpu.SemaphoreType.DMA,
+            pltpu.SemaphoreType.REGULAR((size // RING_X // 2 + RING_X // 2 - 1,)),
         ],
         compiler_params=pltpu.CompilerParams(
-            collective_id=0, has_side_effects=True, vmem_limit_bytes=60 * 1024 * 1024
+            collective_id=0, has_side_effects=True, vmem_limit_bytes=56 * 1024 * 1024
         ),
     )(queries, enc_keys, enc_values, dec_ids, enc_ids)
 

time: 195 us -> 192 us (0.985)
  Pallas kernels: 192 us -> 190 us
    pallas_call x1, Pallas kernels: 192 us -> 190 us  [local(): pl.pallas_call(functools.partial(kernel, size), out_shape=pltpu.VMEM(quer...]
where the time goes in v2:
time: 192 us
  Pallas kernels  190 us (99%)
    pallas_call x1, Pallas kernels, local(): pl.pallas_call(functools.partial(kernel, size), out_shape=pltpu.VMEM(quer...  190 us

profile of v2, /device:TPU:72, one launch (start us, length us, event | category | flops | bytes accessed | tf_op | source)
XLA Modules:
  0.0 191.5 jit_solution(5810489143514860826)
XLA Ops:
  0.0 190.2 %shard_map.55 = bf16[8,64,2048]{2,1,0:T(8,128)(2,1)S(1)} custom-call(bf16[8,64,2048]{2,1,0:T(8,128)(2,1)} %q_ref.1, bf16[8,64,2048]{2,1,0:T(8,128)(2,1)} %k_ref.1, bf16[8,64,2048]{2,1,0:T(8,128)(2,1)} %v_ref.1, s32[8,64]{1,0:T(8,128)} %dec_ref.1, s32[8,64]{1,0:T(8,128)} %enc_ref.1), custom_call_target="tpu_custom_call" | custom-call | tf_op jit(solution)/shard_map/pallas_call | solution.py:236
  190.2 1.3 copy.7

commit v3 on v2

--- a/solution.py
+++ b/solution.py
@@ -95,17 +95,18 @@
         ).start()
 
     def each_at(nearest, farthest, act):
-        def step(o, carry):
-            dz, dx = o // RING_X, lax.rem(o, RING_X)
+        def step(t, carry):
+            dz = lax.rem(t // RING_X - me // RING_X + ring_z, ring_z)
+            dx = lax.rem(lax.rem(t, RING_X) - lax.rem(me, RING_X) + RING_X, RING_X)
             hops = jnp.minimum(dz, ring_z - dz) + jnp.minimum(dx, RING_X - dx)
 
             @pl.when((hops >= nearest) & (hops <= farthest))
             def _():
-                act(place(dz, dx))
+                act(t)
 
             return carry
 
-        lax.fori_loop(1, size, step, 0)
+        lax.fori_loop(0, size, step, 0)
 
     def send_row(r, nearest, farthest):
         for a in range(3):
@@ -113,12 +114,12 @@
 
     pl.semaphore_wait(barrier, 4)
     greet(round_sem.at[0])
-    for t in neighbours:
-        send_counts(t)
     for r in range(rows):
         for a in range(3):
             for t in neighbours:
                 send(t, r, a)
+    for t in neighbours:
+        send_counts(t)
     pl.semaphore_wait(round_sem.at[0], 4)
     greet(round_sem.at[1])
     each_at(2, 2, send_counts)

time: 192 us -> 191 us (level)
  no operation moved by 1% of the time
where the time goes in v3:
time: 191 us
  Pallas kernels  190 us (99%)
    pallas_call x1, Pallas kernels, local(): pl.pallas_call(functools.partial(kernel, size), out_shape=pltpu.VMEM(quer...  190 us

profile of v3, /device:TPU:72, one launch (start us, length us, event | category | flops | bytes accessed | tf_op | source)
XLA Modules:
  0.0 191.1 jit_solution(14191459010931244872)
XLA Ops:
  0.0 189.8 %shard_map.55 = bf16[8,64,2048]{2,1,0:T(8,128)(2,1)S(1)} custom-call(bf16[8,64,2048]{2,1,0:T(8,128)(2,1)} %q_ref.1, bf16[8,64,2048]{2,1,0:T(8,128)(2,1)} %k_ref.1, bf16[8,64,2048]{2,1,0:T(8,128)(2,1)} %v_ref.1, s32[8,64]{1,0:T(8,128)} %dec_ref.1, s32[8,64]{1,0:T(8,128)} %enc_ref.1), custom_call_target="tpu_custom_call" | custom-call | tf_op jit(solution)/shard_map/pallas_call | solution.py:237
  189.8 1.3 copy.7

commit v4 on v3

--- a/solution.py
+++ b/solution.py
@@ -123,7 +123,8 @@
     pl.semaphore_wait(round_sem.at[0], 4)
     greet(round_sem.at[1])
     each_at(2, 2, send_counts)
-    send_row(0, 2, 2)
+    for r in range(rows):
+        send_row(r, 2, 2)
     for k in range(1, rounds):
         pl.semaphore_wait(round_sem.at[k], 4)
         if k + 1 < rounds:
@@ -131,7 +132,7 @@
     each_at(3, size, send_counts)
     send_row(0, 3, size)
     for r in range(1, rows):
-        send_row(r, 2, size)
+        send_row(r, 3, size)
     v_buf[:, :, LANES:] = jnp.ones((rows, length, LANES), jnp.bfloat16)
 
     others = gath.at[pl.ds(0, size - 1)]

time: 191 us -> 191 us (level)
  no operation moved by 1% of the time
where the time goes in v4:
time: 191 us
  Pallas kernels  189 us (99%)
    pallas_call x1, Pallas kernels, local(): pl.pallas_call(functools.partial(kernel, size), out_shape=pltpu.VMEM(quer...  189 us

profile of v4, /device:TPU:72, one launch (start us, length us, event | category | flops | bytes accessed | tf_op | source)
XLA Modules:
  0.0 190.8 jit_solution(16495775585583985812)
XLA Ops:
  0.0 189.5 %shard_map.55 = bf16[8,64,2048]{2,1,0:T(8,128)(2,1)S(1)} custom-call(bf16[8,64,2048]{2,1,0:T(8,128)(2,1)} %q_ref.1, bf16[8,64,2048]{2,1,0:T(8,128)(2,1)} %k_ref.1, bf16[8,64,2048]{2,1,0:T(8,128)(2,1)} %v_ref.1, s32[8,64]{1,0:T(8,128)} %dec_ref.1, s32[8,64]{1,0:T(8,128)} %enc_ref.1), custom_call_target="tpu_custom_call" | custom-call | tf_op jit(solution)/shard_map/pallas_call | solution.py:238
  189.5 1.3 copy.7

commit v5 on v4

--- a/solution.py
+++ b/solution.py
@@ -123,8 +123,7 @@
     pl.semaphore_wait(round_sem.at[0], 4)
     greet(round_sem.at[1])
     each_at(2, 2, send_counts)
-    for r in range(rows):
-        send_row(r, 2, 2)
+    each_at(2, 2, lambda t: [send(t, r, a) for r in range(rows) for a in range(3)])
     for k in range(1, rounds):
         pl.semaphore_wait(round_sem.at[k], 4)
         if k + 1 < rounds:

time: 191 us -> 192 us (level)
  Pallas kernels: 189 us -> 191 us
where the time goes in v5:
time: 192 us
  Pallas kernels  191 us (99%)
    pallas_call x1, Pallas kernels, local(): pl.pallas_call(functools.partial(kernel, size), out_shape=pltpu.VMEM(quer...  191 us

profile of v5, /device:TPU:72, one launch (start us, length us, event | category | flops | bytes accessed | tf_op | source)
XLA Modules:
  0.0 192.3 jit_solution(17003581937888891589)
XLA Ops:
  0.0 191.0 %shard_map.55 = bf16[8,64,2048]{2,1,0:T(8,128)(2,1)S(1)} custom-call(bf16[8,64,2048]{2,1,0:T(8,128)(2,1)} %q_ref.1, bf16[8,64,2048]{2,1,0:T(8,128)(2,1)} %k_ref.1, bf16[8,64,2048]{2,1,0:T(8,128)(2,1)} %v_ref.1, s32[8,64]{1,0:T(8,128)} %dec_ref.1, s32[8,64]{1,0:T(8,128)} %enc_ref.1), custom_call_target="tpu_custom_call" | custom-call | tf_op jit(solution)/shard_map/pallas_call | solution.py:237
  191.0 1.3 copy.7
